TPU v7x, 32 devices: a whole 2x2x4 slice. The times are simulated.
32 devices in a mesh: fsdp: 8 (over y, x, core), tp: 4 (over z).
Axes of the slice: x: 2, y: 2, z: 4, core: 2. Of those that a mesh axis runs over, the one named last changes fastest.
Arguments:
- inputs: float32 [8192, 768], P(('fsdp', 'tp')), may hold values from -6 to 6
- out_cotangent: float32 [8192, 768], P('fsdp'), may hold values from -6 to 6
- clip_lengths: int32 [6], replicated, may hold values from 384 to 1536, as said below
- norm1_gain: float32 [768], replicated, may hold values from 0.5 to 1.5
- norm1_shift: float32 [768], replicated, may hold values from -3 to 3
- query_weight: bfloat16 [768, 768], P('fsdp', 'tp'), may hold values from -0.21875 to 0.21875
- query_bias: float32 [768], replicated, may hold values from -3 to 3
- key_weight: bfloat16 [768, 768], P('fsdp', 'tp'), may hold values from -0.21875 to 0.21875
- value_weight: bfloat16 [768, 768], P('fsdp', 'tp'), may hold values from -0.21875 to 0.21875
- value_bias: float32 [768], replicated, may hold values from -3 to 3
- out_weight: bfloat16 [768, 768], P('fsdp', 'tp'), may hold values from -0.75 to 0.75
- out_bias: float32 [768], replicated, may hold values from -3 to 3
- norm2_gain: float32 [768], replicated, may hold values from 0.5 to 1.5
- norm2_shift: float32 [768], replicated, may hold values from -3 to 3
- fc1_weight: bfloat16 [3072, 768], P(('fsdp', 'tp')), may hold values from -0.21875 to 0.21875
- fc1_bias: float32 [3072], replicated, may hold values from -3 to 3
- fc2_weight: bfloat16 [3072, 768], P(('fsdp', 'tp')), may hold values from -0.3125 to 0.3125
- fc2_bias: float32 [768], replicated, may hold values from -3 to 3
Outputs:
- outputs: float32 [8192, 768], P(('fsdp', 'tp'))
- inputs_grad: float32 [8192, 768], P(('fsdp', 'tp'))
- norm1_gain_grad: float32 [768], replicated
- norm1_shift_grad: float32 [768], replicated
- query_weight_grad: float32 [768, 768], P('fsdp', 'tp')
- query_bias_grad: float32 [768], replicated
- key_weight_grad: float32 [768, 768], P('fsdp', 'tp')
- value_weight_grad: float32 [768, 768], P('fsdp', 'tp')
- value_bias_grad: float32 [768], replicated
- out_weight_grad: float32 [768, 768], P('fsdp', 'tp')
- out_bias_grad: float32 [768], replicated
- norm2_gain_grad: float32 [768], replicated
- norm2_shift_grad: float32 [768], replicated
- fc1_weight_grad: float32 [3072, 768], P(('fsdp', 'tp'))
- fc1_bias_grad: float32 [3072], replicated
- fc2_weight_grad: float32 [3072, 768], P(('fsdp', 'tp'))
- fc2_bias_grad: float32 [768], replicated
Inputs may be any that keep to these rules, and one draw needn't show every extreme that they name: `clip_lengths`: clip c has at most min(1536, 8192 - c * 1536) valid frames; some clip has all 1536 frames valid.
All inputs are finite; a program needn't handle non-finite values.
Results may differ from a plain program's by a relative error of at most 0.03.
Values may be sent and summed in bfloat16 or wider, within the bound.
A program may use at most 128 MiB of HBM per device.

v0:
```python
import math
import jax
import jax.numpy as jnp
from jax import lax
from jax.sharding import PartitionSpec as P

HD = 64
CLIP = 1536
QB = 512
eps_norm = 1e-05
root_half = 0.7071067811865476
inv_root_tau = 0.3989422804014327
far_negative = -1e30


def extended(value, sides, width):
    for axis, dim in sides:
        size, length = (lax.axis_size(axis), value.shape[dim])
        up = [(i, (i + 1) % size) for i in range(size - 1)]
        down = [(j, i) for i, j in up]
        last = lax.slice_in_dim(value, length - width, length, axis=dim)
        initial = lax.slice_in_dim(value, 0, width, axis=dim)
        before = lax.ppermute(last, axis, up)
        after = lax.ppermute(initial, axis, down)
        value = jnp.concatenate([before, value, after], axis=dim)
    return value


def normalize(rows, gain, shift):
    centre = jnp.mean(rows, axis=-1, keepdims=True)
    centred = rows - centre
    inv_spread = lax.rsqrt(jnp.mean(centred * centred, axis=-1, keepdims=True) + eps_norm)
    unit_rows = centred * inv_spread
    return (unit_rows, inv_spread, unit_rows * gain + shift)


def norm_back(upstream, unit_rows, inv_spread, gain):
    scaled = upstream * gain
    return inv_spread * (
        scaled
        - jnp.mean(scaled, axis=-1, keepdims=True)
        - unit_rows * jnp.mean(scaled * unit_rows, axis=-1, keepdims=True)
    )


def gelu_exact(values):
    return 0.5 * values * (1.0 + lax.erf(values * root_half))


def gelu_slope(values):
    return (
        0.5 * (1.0 + lax.erf(values * root_half))
        + values * jnp.exp(-0.5 * values * values) * inv_root_tau
    )


def contract_rows(left_rows, right_rows):
    return lax.dot_general(
        left_rows, right_rows, (((0,), (0,)), ((), ())), preferred_element_type=jnp.float32
    )


def contract_cols(left_rows, right_rows):
    return lax.dot_general(
        left_rows, right_rows, (((1,), (1,)), ((), ())), preferred_element_type=jnp.float32
    )


def fetch_attention(query_weight, key_weight, value_weight, out_weight):
    return (
        lax.all_gather(query_weight, "fsdp", axis=0, tiled=True),
        lax.all_gather(key_weight, "fsdp", axis=0, tiled=True),
        lax.all_gather(value_weight, "fsdp", axis=0, tiled=True),
        lax.all_gather(out_weight, "fsdp", axis=0, tiled=True),
    )


def on_device(
    inputs,
    out_cotangent,
    clip_lengths,
    norm1_gain,
    norm1_shift,
    query_weight,
    query_bias,
    key_weight,
    value_weight,
    value_bias,
    out_weight,
    out_bias,
    norm2_gain,
    norm2_shift,
    fc1_weight,
    fc1_bias,
    fc2_weight,
    fc2_bias,
):
    bf16 = jnp.bfloat16
    f32 = jnp.float32
    tp_count = lax.axis_size("tp")
    fsdp_count = lax.axis_size("fsdp")
    tp_index = lax.axis_index("tp")
    fsdp_index = lax.axis_index("fsdp")
    own_rows = inputs.shape[0]
    group_rows = out_cotangent.shape[0]
    score_scale = 1.0 / math.sqrt(HD)
    margin = CLIP - QB
    tp_slot = (jnp.arange(tp_count) == tp_index).astype(f32)
    own_cotangent = lax.dynamic_slice_in_dim(out_cotangent, tp_index * own_rows, own_rows, 0)
    unit1, spread1, normed_own = normalize(inputs, norm1_gain, norm1_shift)
    normed = lax.all_gather(normed_own.astype(bf16), "tp", axis=0, tiled=True)
    query_w, key_w, value_w, out_w = fetch_attention(
        query_weight, key_weight, value_weight, out_weight
    )
    local_width = query_w.shape[1]
    heads_here = local_width // HD
    column_start = tp_index * local_width
    query = (
        jnp.dot(normed, query_w, preferred_element_type=f32)
        + lax.dynamic_slice_in_dim(query_bias, column_start, local_width, 0)
    ).astype(bf16)
    key = jnp.dot(normed, key_w, preferred_element_type=f32).astype(bf16)
    value = (
        jnp.dot(normed, value_w, preferred_element_type=f32)
        + lax.dynamic_slice_in_dim(value_bias, column_start, local_width, 0)
    ).astype(bf16)
    padded = extended(jnp.stack([key, value]), (("fsdp", 1),), margin)
    group_base = fsdp_index * group_rows
    clip_ids = jnp.arange(clip_lengths.shape[0])
    block_count = group_rows // QB

    def block_scores(block_index):
        first_row = block_index * QB
        clip_index = (group_base + first_row) // CLIP
        key_start = clip_index * CLIP - group_base + margin
        length = jnp.sum(jnp.where(clip_ids == clip_index, clip_lengths, 0))
        query_block = lax.dynamic_slice_in_dim(query, first_row, QB, 0).reshape(QB, heads_here, HD)
        pair = lax.dynamic_slice_in_dim(padded, key_start, CLIP, 1).reshape(2, CLIP, heads_here, HD)
        scores = (
            jnp.einsum("qhe,khe->hqk", query_block, pair[0], preferred_element_type=f32)
            * score_scale
        )
        scores = jnp.where((jnp.arange(CLIP) < length)[None, None, :], scores, far_negative)
        return (first_row, key_start, query_block, pair[0], pair[1], scores)

    def attend(block_index, carry):
        context_rows, total_rows = carry
        first_row, key_start, query_block, key_block, value_block, scores = block_scores(
            block_index
        )
        highest = jnp.max(scores, axis=-1, keepdims=True)
        log_total = highest[..., 0] + jnp.log(jnp.sum(jnp.exp(scores - highest), axis=-1))
        weights = jnp.exp(scores - log_total[..., None]).astype(bf16)
        block_out = jnp.einsum("hqk,khe->qhe", weights, value_block, preferred_element_type=f32)
        block_out = block_out.astype(bf16).reshape(QB, local_width)
        context_rows = lax.dynamic_update_slice_in_dim(context_rows, block_out, first_row, 0)
        total_rows = lax.dynamic_update_slice_in_dim(total_rows, log_total, first_row, 1)
        return (context_rows, total_rows)

    context, totals = lax.fori_loop(
        0,
        block_count,
        attend,
        (jnp.zeros((group_rows, local_width), bf16), jnp.zeros((heads_here, group_rows), f32)),
    )
    attended = lax.psum_scatter(
        contract_cols(context, out_w), "tp", scatter_dimension=0, tiled=True
    )
    hidden = inputs + attended + out_bias
    unit2, spread2, normed2_full = normalize(hidden, norm2_gain, norm2_shift)
    normed2_own = normed2_full.astype(bf16)
    normed2 = lax.all_gather(normed2_own, "tp", axis=0, tiled=True)
    w_up, w_down = (
        lax.all_gather(fc1_weight, "fsdp", axis=0, tiled=True),
        lax.all_gather(fc2_weight, "fsdp", axis=0, tiled=True),
    )
    unit_count = fc1_weight.shape[0]
    bias_up = lax.dynamic_index_in_dim(
        fc1_bias.reshape(fsdp_count, tp_count, unit_count), tp_index, 1, False
    ).reshape(-1)
    preact = contract_cols(normed2, w_up) + bias_up
    activated = gelu_exact(preact).astype(bf16)
    mixed = lax.psum_scatter(
        jnp.dot(activated, w_down, preferred_element_type=f32),
        "tp",
        scatter_dimension=0,
        tiled=True,
    )
    outputs = hidden + mixed + fc2_bias
    up_rounded = out_cotangent.astype(bf16)
    dactivated = contract_cols(up_rounded, w_down)
    dpreact = (dactivated * gelu_slope(preact)).astype(bf16)
    grad_up_part = contract_rows(dpreact, normed2)
    grad_down_part = contract_rows(activated, up_rounded)
    upbias_part = jnp.sum(dpreact.astype(f32), axis=0)
    grad_b1 = (upbias_part.reshape(fsdp_count, 1, unit_count) * tp_slot[None, :, None]).reshape(-1)
    dnorm2 = lax.psum_scatter(
        jnp.dot(dpreact, w_up, preferred_element_type=f32), "tp", scatter_dimension=0, tiled=True
    )
    grad_fc1, grad_fc2 = (
        lax.psum_scatter(grad_up_part, "fsdp", scatter_dimension=0, tiled=True),
        lax.psum_scatter(grad_down_part, "fsdp", scatter_dimension=0, tiled=True),
    )
    grad_b2 = jnp.sum(own_cotangent, axis=0)
    grad_gain2 = jnp.sum(dnorm2 * unit2, axis=0)
    grad_shift2 = jnp.sum(dnorm2, axis=0)
    dhidden = own_cotangent + norm_back(dnorm2, unit2, spread2, norm2_gain)
    grad_obias = jnp.sum(dhidden, axis=0)
    query_w, key_w, value_w, out_w = fetch_attention(
        query_weight, key_weight, value_weight, out_weight
    )
    dh_all = lax.all_gather(dhidden.astype(bf16), "tp", axis=0, tiled=True)
    dcontext = jnp.dot(dh_all, out_w, preferred_element_type=f32).astype(bf16)
    grad_out = contract_rows(dh_all, context)
    delta = jnp.sum(
        (dcontext.astype(f32) * context.astype(f32)).reshape(group_rows, heads_here, HD), axis=-1
    ).T

    def attend_back(block_index, carry):
        dquery_rows, dpair = carry
        first_row, key_start, query_block, key_block, value_block, scores = block_scores(
            block_index
        )
        grad_block = lax.dynamic_slice_in_dim(dcontext, first_row, QB, 0).reshape(
            QB, heads_here, HD
        )
        probs = jnp.exp(scores - lax.dynamic_slice_in_dim(totals, first_row, QB, 1)[..., None])
        delta_block = lax.dynamic_slice_in_dim(delta, first_row, QB, 1)
        dprobs = jnp.einsum("qhe,khe->hqk", grad_block, value_block, preferred_element_type=f32)
        dscores = (probs * (dprobs - delta_block[..., None]) * score_scale).astype(bf16)
        dquery_block = jnp.einsum("hqk,khe->qhe", dscores, key_block, preferred_element_type=f32)
        dquery_block = dquery_block.astype(bf16).reshape(QB, local_width)
        dkey_block = jnp.einsum(
            "hqk,qhe->khe", dscores, query_block, preferred_element_type=f32
        ).reshape(CLIP, local_width)
        dvalue_block = jnp.einsum(
            "hqk,qhe->khe", probs.astype(bf16), grad_block, preferred_element_type=f32
        ).reshape(CLIP, local_width)
        current = lax.dynamic_slice_in_dim(dpair, key_start, CLIP, 1)
        dpair = lax.dynamic_update_slice_in_dim(
            dpair, current + jnp.stack([dkey_block, dvalue_block]), key_start, 1
        )
        dquery_rows = lax.dynamic_update_slice_in_dim(dquery_rows, dquery_block, first_row, 0)
        return (dquery_rows, dpair)

    dquery, dpair = lax.fori_loop(
        0,
        block_count,
        attend_back,
        (jnp.zeros((group_rows, local_width), bf16), jnp.zeros(padded.shape, f32)),
    )
    rims = jnp.concatenate([dpair[:, :margin], dpair[:, margin + group_rows :]], axis=1)
    received = extended(rims, (("fsdp", 1),), margin)
    inner_part = dpair[:, margin : margin + group_rows]
    inner_part = inner_part.at[:, :margin].add(received[:, :margin])
    inner_part = inner_part.at[:, group_rows - margin :].add(received[:, 3 * margin :])
    dkey = inner_part[0].astype(bf16)
    dvalue = inner_part[1].astype(bf16)
    grad_query = contract_rows(normed, dquery)
    grad_key = contract_rows(normed, dkey)
    grad_value = contract_rows(normed, dvalue)
    grad_qbias = (tp_slot[:, None] * jnp.sum(dquery.astype(f32), axis=0)[None, :]).reshape(-1)
    grad_vbias = (tp_slot[:, None] * jnp.sum(dvalue.astype(f32), axis=0)[None, :]).reshape(-1)
    dnorm1 = lax.psum_scatter(
        contract_cols(dquery, query_w)
        + contract_cols(dkey, key_w)
        + contract_cols(dvalue, value_w),
        "tp",
        scatter_dimension=0,
        tiled=True,
    )
    grad_gain1 = jnp.sum(dnorm1 * unit1, axis=0)
    grad_shift1 = jnp.sum(dnorm1, axis=0)
    inputs_grad = dhidden + norm_back(dnorm1, unit1, spread1, norm1_gain)
    grad_query, grad_key, grad_value, grad_out = (
        lax.psum_scatter(grad_query, "fsdp", scatter_dimension=0, tiled=True),
        lax.psum_scatter(grad_key, "fsdp", scatter_dimension=0, tiled=True),
        lax.psum_scatter(grad_value, "fsdp", scatter_dimension=0, tiled=True),
        lax.psum_scatter(grad_out, "fsdp", scatter_dimension=0, tiled=True),
    )
    (
        grad_gain1,
        grad_shift1,
        grad_qbias,
        grad_vbias,
        grad_obias,
        grad_gain2,
        grad_shift2,
        grad_b1,
        grad_b2,
    ) = lax.psum(
        (
            grad_gain1,
            grad_shift1,
            grad_qbias,
            grad_vbias,
            grad_obias,
            grad_gain2,
            grad_shift2,
            grad_b1,
            grad_b2,
        ),
        ("fsdp", "tp"),
    )
    return (
        outputs,
        inputs_grad,
        grad_gain1,
        grad_shift1,
        grad_query,
        grad_qbias,
        grad_key,
        grad_value,
        grad_vbias,
        grad_out,
        grad_obias,
        grad_gain2,
        grad_shift2,
        grad_fc1,
        grad_b1,
        grad_fc2,
        grad_b2,
    )


def solution(mesh):
    in_specs = (
        P(("fsdp", "tp"), None),
        P("fsdp", None),
        P(),
        P(),
        P(),
        P("fsdp", "tp"),
        P(),
        P("fsdp", "tp"),
        P("fsdp", "tp"),
        P(),
        P("fsdp", "tp"),
        P(),
        P(),
        P(),
        P(("fsdp", "tp"), None),
        P(),
        P(("fsdp", "tp"), None),
        P(),
    )
    out_specs = (
        P(("fsdp", "tp"), None),
        P(("fsdp", "tp"), None),
        P(),
        P(),
        P("fsdp", "tp"),
        P(),
        P("fsdp", "tp"),
        P("fsdp", "tp"),
        P(),
        P("fsdp", "tp"),
        P(),
        P(),
        P(),
        P(("fsdp", "tp"), None),
        P(),
        P(("fsdp", "tp"), None),
        P(),
    )
    return jax.shard_map(
        on_device, mesh=mesh, in_specs=in_specs, out_specs=out_specs, check_vma=False
    )
```

profile of v0, /device:TPU:0, one launch (start us, length us, event | category | flops | bytes accessed | tf_op | source)
XLA Modules:
  0.0 818.0 jit_solution(7291975622718793777)
XLA Ops:
  13.7 11.0 %all_gather.32 = bf16[768,192]{1,0:T(8,128)(2,1)S(1)} all-gather(bf16[96,192]{1,0:T(8,128)(2,1)S(1)} %copy-done.22), channel_id=1, replica_groups=mesh['fsdp'=8,'tp'=4] {'fsdp'}, dimensions={0}, use_global_device_ids=true | all-gather | bytes 331776 | tf_op jit(solution)/shard_map/all_gather | solution.py:72
  24.7 9.5 %all_gather.33 = bf16[768,192]{1,0:T(8,128)(2,1)S(1)} all-gather(bf16[96,192]{1,0:T(8,128)(2,1)S(1)} %copy-done.23), channel_id=1, replica_groups=mesh['fsdp'=8,'tp'=4] {'fsdp'}, dimensions={0}, use_global_device_ids=true | all-gather | bytes 331776 | tf_op jit(solution)/shard_map/all_gather | solution.py:73
  34.3 18.5 %all-gather.6.cloned.1.call-done = bf16[1024,768]{1,0:T(8,128)(2,1)} async-done(((bf16[256,768]{1,0:T(8,128)(2,1)}), bf16[1024,768]{1,0:T(8,128)(2,1)}) %all-gather.6.cloned.1.call-update) | async-done | bytes 1572880 | tf_op jit(solution)/shard_map/all_gather | solution.py:111
  59.3 4.0 collective-permute-start
  64.0 18.6 %all_gather.34 = bf16[768,192]{1,0:T(8,128)(2,1)S(1)} all-gather(bf16[96,192]{1,0:T(8,128)(2,1)S(1)} %copy-done.24), channel_id=1, replica_groups=mesh['fsdp'=8,'tp'=4] {'fsdp'}, dimensions={0}, use_global_device_ids=true | all-gather | bytes 331776 | tf_op jit(solution)/shard_map/all_gather | solution.py:71
  82.6 11.4 %all_gather.35 = bf16[768,192]{1,0:T(8,128)(2,1)} all-gather(bf16[96,192]{1,0:T(8,128)(2,1)S(1)} %copy-done.25), channel_id=1, replica_groups=mesh['fsdp'=8,'tp'=4] {'fsdp'}, dimensions={0}, use_global_device_ids=true | all-gather | bytes 331776 | tf_op jit(solution)/shard_map/all_gather | solution.py:74
  97.1 17.5 %while.40 = (s32[]{:T(128)}, bf16[1024,192]{0,1:T(8,128)(2,1)}, f32[3,1024]{1,0:T(4,128)S(1)}, s32[]{:T(128)}, bf16[2,3072,192]{1,2,0:T(8,128)(2,1)S(1)}, /*inde...) while((s32[]{:T(128)}, bf16[1024,192]{0,1:T(8,128)(2,1)}, ...), condition=%wide.region_6.7_spmd.clone, body=%wide.region_2.6_spmd.clone.sunk | while | flops 630030336 | bytes 36239832 | solution.py:160
  114.6 3.5 fusion.40
  118.7 58.8 %reduce-scatter.11.cloned.1.call-done = f32[256,768]{1,0:T(8,128)} async-done(((f32[1024,768]{1,0:T(8,128)}), f32[256,768]{1,0:T(8,128)}) %reduce-scatter.11.cloned.1.call-update) | async-done | bytes 786448 | tf_op jit(solution)/shard_map/reduce_scatter | solution.py:166
  184.3 33.2 %all-gather.8.cloned.1.call-done = bf16[1024,768]{1,0:T(8,128)(2,1)} async-done(((bf16[256,768]{1,0:T(8,128)(2,1)}), bf16[1024,768]{1,0:T(8,128)(2,1)}) %all-gather.8.cloned.1.call-update) | async-done | bytes 1572880 | tf_op jit(solution)/shard_map/all_gather | solution.py:172
  217.6 5.4 multiply_convert_fusion.1
  223.0 19.1 %all-gather.12.cloned.1.call-done = bf16[768,768]{1,0:T(8,128)(2,1)} async-done(((bf16[96,768]{1,0:T(8,128)(2,1)}), bf16[768,768]{1,0:T(8,128)(2,1)}) %all-gather.12.cloned.1.call-update) | async-done | bytes 1179664 | tf_op jit(solution)/shard_map/all_gather | solution.py:175
  242.1 6.1 convert_reduce_fusion
  252.5 4.8 fusion.41
  257.4 55.6 %reduce-scatter.15.cloned.1.call-done = f32[256,768]{1,0:T(8,128)} async-done(((f32[1024,768]{1,0:T(8,128)}), f32[256,768]{1,0:T(8,128)}) %reduce-scatter.15.cloned.1.call-update) | async-done | bytes 786448 | tf_op jit(solution)/shard_map/reduce_scatter | solution.py:197
  315.9 59.7 %reduce-scatter.13.cloned.1.call-done = f32[256,768]{1,0:T(8,128)} async-done(((f32[1024,768]{1,0:T(8,128)}), f32[256,768]{1,0:T(8,128)}) %reduce-scatter.13.cloned.1.call-update) | async-done | bytes 786448 | tf_op jit(solution)/shard_map/reduce_scatter | solution.py:183
  375.5 3.7 fusion.35
  381.2 36.8 %all-gather.14.cloned.1.call-done = bf16[1024,768]{1,0:T(8,128)(2,1)} async-done(((bf16[256,768]{1,0:T(8,128)(2,1)}), bf16[1024,768]{1,0:T(8,128)(2,1)}) %all-gather.14.cloned.1.call-update) | async-done | bytes 1572880 | tf_op jit(solution)/shard_map/all_gather | solution.py:212
  418.0 3.3 convert_multiply_fusion
  425.9 32.3 %while.41 = (s32[]{:T(128)}, bf16[1024,192]{0,1:T(8,128)(2,1)}, f32[2,3072,192]{1,2,0:T(8,128)}, s32[]{:T(128)}, bf16[2,3072,192]{1,2,0:T(8,128)(2,1)S(1)}, /*in...) while((s32[]{:T(128)}, bf16[1024,192]{0,1:T(8,128)(2,1)}, ...), condition=%wide.region_17.18_spmd.clone, body=%wide.region_15.17_spmd.clone.sunk | while | flops 1537181184 | bytes 94420032 | solution.py:246
  433.2 3.4 multiply_convert_fusion.3
  449.3 3.4 multiply_convert_fusion.3
  464.7 4.0 collective-permute-done.3
  475.5 4.3 fusion.46
  480.2 5.2 fusion.29
  499.4 63.9 %reduce-scatter.17.cloned.1.call-done = f32[256,768]{1,0:T(8,128)} async-done(((f32[1024,768]{1,0:T(8,128)}), f32[256,768]{1,0:T(8,128)}) %reduce-scatter.17.cloned.1.call-update) | async-done | bytes 786448 | tf_op jit(solution)/shard_map/reduce_scatter | solution.py:264
  564.9 41.5 %all-reduce = (f32[768]{0:T(1024)}, f32[768]{0:T(1024)}, f32[768]{0:T(1024)}, f32[768]{0:T(1024)}, f32[768]{0:T(1024)}, /*index=5*/f32[768]{0:T(1024)}, f32[768]{0:T(1024)}, f32[3072]{0:T(1024)}, f32[768]{0:T(1024)}) all-reduce(f32[768]{0:T(1024)S(1)} %get-tuple-element.569, ...), channel_id=1, replica_groups=mesh['fsdp'=8,'tp'=4] {'fsdp','tp'}, use_global_device_ids=true, to_apply=%region_22.23 | all-reduce | flops 9216 | bytes 73728 | tf_op jit(solution)/shard_map/psum | solution.py:291
  609.5 46.3 %reduce-scatter.29.cloned.1.call-done = f32[96,768]{1,0:T(8,128)} async-done(((f32[768,768]{1,0:T(8,128)}), f32[96,768]{1,0:T(8,128)}) %reduce-scatter.29.cloned.1.call-update) | async-done | bytes 294928 | tf_op jit(solution)/shard_map/reduce_scatter | solution.py:202
  655.8 38.7 %reduce-scatter.25.cloned.1.call-done = f32[96,192]{1,0:T(8,128)} async-done(((f32[768,192]{1,0:T(8,128)}), f32[96,192]{1,0:T(8,128)}) %reduce-scatter.25.cloned.1.call-update) | async-done | bytes 73744 | tf_op jit(solution)/shard_map/reduce_scatter | solution.py:279
  694.5 38.7 %reduce-scatter.19.cloned.1.call-done = f32[96,192]{1,0:T(8,128)} async-done(((f32[768,192]{1,0:T(8,128)}), f32[96,192]{1,0:T(8,128)}) %reduce-scatter.19.cloned.1.call-update) | async-done | bytes 73744 | tf_op jit(solution)/shard_map/reduce_scatter | solution.py:276
  733.2 38.7 %reduce-scatter.21.cloned.1.call-done = f32[96,192]{1,0:T(8,128)} async-done(((f32[768,192]{1,0:T(8,128)}), f32[96,192]{1,0:T(8,128)}) %reduce-scatter.21.cloned.1.call-update) | async-done | bytes 73744 | tf_op jit(solution)/shard_map/reduce_scatter | solution.py:277
  771.9 38.6 %reduce-scatter.23.cloned.1.call-done = f32[96,192]{1,0:T(8,128)} async-done(((f32[768,192]{1,0:T(8,128)}), f32[96,192]{1,0:T(8,128)}) %reduce-scatter.23.cloned.1.call-update) | async-done | bytes 73744 | tf_op jit(solution)/shard_map/reduce_scatter | solution.py:278
  (235 shorter events, 111.7 us)
Async XLA Ops:
  8.0 44.7 %all-gather.6.cloned.1.call-start = ((), (), s32[]{:S(2)}) async-start(), calls=%async_computation.10 | async-start | bytes 1966080 | tf_op jit(solution)/shard_map/all_gather | solution.py:111
  12.9 164.7 %reduce-scatter.11.cloned.1.call-start = ((), (), s32[]{:S(2)}) async-start(), calls=%async_computation.11 | async-start | bytes 3932160 | tf_op jit(solution)/shard_map/reduce_scatter | solution.py:166
  58.0 36.7 %collective-permute-start.1 = (bf16[2,1024,192]{1,2,0:T(8,128)(2,1)}, bf16[2,1024,192]{1,2,0:T(8,128)(2,1)}, u32[]{:S(2)}, u32[]{:S(2)}) collective-permute-start(bf16[2,1024,192]{1,2,0:T(8,128)(2,1)} %pad_maximum_fusion.1), channel_id=1, source_target_pairs={{4,0},{8,4},{12,8},{16,12},{20,16},{24,20},{28,24},{5,1},{9,5},{13... | collective-permute-start | bytes 2359304 | tf_op jit(solution)/shard_map/ppermute | solution.py:24
  59.3 35.4 %collective-permute-start = (bf16[2,1024,192]{1,2,0:T(8,128)(2,1)}, bf16[2,1024,192]{1,2,0:T(8,128)(2,1)}, u32[]{:S(2)}, u32[]{:S(2)}) collective-permute-start(bf16[2,1024,192]{1,2,0:T(8,128)(2,1)} %pad_maximum_fusion.1), channel_id=1, source_target_pairs={{0,4},{4,8},{8,12},{12,16},{16,20},{20,24},{24,28},{1,5},{5,9},{9,... | collective-permute-start | bytes 2359304 | tf_op jit(solution)/shard_map/ppermute | solution.py:23
  114.6 63.0 %copy-start.1 = (f32[256,768]{1,0:T(8,128)S(1)}, f32[256,768]{1,0:T(8,128)}, u32[]{:S(2)}) copy-start(f32[256,768]{1,0:T(8,128)} %param.30) | copy-start | bytes 2359300
  118.1 66.3 %all-gather.10.cloned.1.call-start = ((), (), s32[]{:S(2)}) async-start(), calls=%async_computation.13 | async-start | bytes 1327104 | tf_op jit(solution)/shard_map/all_gather | solution.py:174
  118.1 61.6 %copy-start.28 = (f32[768]{0:T(1024)S(1)}, f32[768]{0:T(1024)}, u32[]{:S(2)}) copy-start(f32[768]{0:T(1024)} %param.42) | copy-start | bytes 9220
  118.1 61.6 %copy-start.37 = (f32[768]{0:T(1024)S(1)}, f32[768]{0:T(1024)}, u32[]{:S(2)}) copy-start(f32[768]{0:T(1024)} %param.43) | copy-start | bytes 9220
  118.7 98.9 %all-gather.8.cloned.1.call-start = ((), (), s32[]{:S(2)}) async-start(), calls=%async_computation.12 | async-start | bytes 1966080 | tf_op jit(solution)/shard_map/all_gather | solution.py:172
  180.7 61.4 %all-gather.12.cloned.1.call-start = ((), (), s32[]{:S(2)}) async-start(), calls=%async_computation.14 | async-start | bytes 1327104 | tf_op jit(solution)/shard_map/all_gather | solution.py:175
  181.3 131.6 %reduce-scatter.15.cloned.1.call-start = ((), (), s32[]{:S(2)}) async-start(), calls=%async_computation.16 | async-start | bytes 3932160 | tf_op jit(solution)/shard_map/reduce_scatter | solution.py:197
  184.3 57.8 %copy-start.39 = (f32[768]{0:T(1024)S(1)}, f32[768]{0:T(1024)}, u32[]{:S(2)}) copy-start(f32[768]{0:T(1024)} %add.362) | copy-start | bytes 9220
  252.4 123.1 %reduce-scatter.13.cloned.1.call-start = ((), (), s32[]{:S(2)}) async-start(), calls=%async_computation.15 | async-start | bytes 3932160 | tf_op jit(solution)/shard_map/reduce_scatter | solution.py:183
  257.3 160.7 %all-gather.14.cloned.1.call-start = ((), (), s32[]{:S(2)}) async-start(), calls=%async_computation.17 | async-start | bytes 1966080 | tf_op jit(solution)/shard_map/all_gather | solution.py:212
  380.9 182.4 %reduce-scatter.17.cloned.1.call-start = ((), (), s32[]{:S(2)}) async-start(), calls=%async_computation.18 | async-start | bytes 3932160 | tf_op jit(solution)/shard_map/reduce_scatter | solution.py:264
  460.4 4.3 collective-permute-start.2
  461.8 6.9 collective-permute-start.3
  474.1 135.3 %reduce-scatter.27.cloned.1.call-start = ((), (), s32[]{:S(2)}) async-start(), calls=%async_computation.23 | async-start | bytes 2654208 | tf_op jit(solution)/shard_map/reduce_scatter | solution.py:201
  479.9 175.9 %reduce-scatter.29.cloned.1.call-start = ((), (), s32[]{:S(2)}) async-start(), calls=%async_computation.24 | async-start | bytes 2654208 | tf_op jit(solution)/shard_map/reduce_scatter | solution.py:202
  485.4 209.1 %reduce-scatter.25.cloned.1.call-start = ((), (), s32[]{:S(2)}) async-start(), calls=%async_computation.22 | async-start | bytes 884736 | tf_op jit(solution)/shard_map/reduce_scatter | solution.py:279
  488.5 244.7 %reduce-scatter.19.cloned.1.call-start = ((), (), s32[]{:S(2)}) async-start(), calls=%async_computation.19 | async-start | bytes 884736 | tf_op jit(solution)/shard_map/reduce_scatter | solution.py:276
  490.2 281.7 %reduce-scatter.21.cloned.1.call-start = ((), (), s32[]{:S(2)}) async-start(), calls=%async_computation.20 | async-start | bytes 884736 | tf_op jit(solution)/shard_map/reduce_scatter | solution.py:277
  493.0 113.4 %copy-start.6 = (f32[256,768]{1,0:T(8,128)S(1)}, f32[256,768]{1,0:T(8,128)}, u32[]{:S(2)}) copy-start(f32[256,768]{1,0:T(8,128)} %copy-done.5) | copy-start | bytes 2359300
  493.1 317.4 %reduce-scatter.23.cloned.1.call-start = ((), (), s32[]{:S(2)}) async-start(), calls=%async_computation.21 | async-start | bytes 884736 | tf_op jit(solution)/shard_map/reduce_scatter | solution.py:278
  494.6 68.7 %copy-start.27 = (f32[768]{0:T(1024)S(1)}, f32[768]{0:T(1024)}, u32[]{:S(2)}) copy-start(f32[768]{0:T(1024)} %param.33) | copy-start | bytes 9220
  494.6 70.2 %copy-start.26 = (f32[3072]{0:T(1024)S(1)}, f32[3072]{0:T(1024)}, u32[]{:S(2)}) copy-start(f32[3072]{0:T(1024)} %mul.315) | copy-start | bytes 36868
  494.8 68.5 %copy-start.30 = (f32[256]{0:T(256)S(1)}, f32[256]{0:T(256)}, u32[]{:S(2)}) copy-start(f32[256]{0:T(256)} %copy-done.29) | copy-start | bytes 3076
  494.8 68.5 %copy-start.32 = (f32[256]{0:T(256)S(1)}, f32[256]{0:T(256)}, u32[]{:S(2)}) copy-start(f32[256]{0:T(256)} %copy-done.31) | copy-start | bytes 3076
  494.8 70.1 %copy-start.33 = (f32[768]{0:T(1024)S(1)}, f32[768]{0:T(1024)}, u32[]{:S(2)}) copy-start(f32[768]{0:T(1024)} %get-tuple-element.567) | copy-start | bytes 9220
  494.8 70.1 %copy-start.34 = (f32[768]{0:T(1024)S(1)}, f32[768]{0:T(1024)}, u32[]{:S(2)}) copy-start(f32[768]{0:T(1024)} %get-tuple-element.573) | copy-start | bytes 9220
  494.8 70.1 %copy-start.35 = (f32[768]{0:T(1024)S(1)}, f32[768]{0:T(1024)}, u32[]{:S(2)}) copy-start(f32[768]{0:T(1024)} %get-tuple-element.620) | copy-start | bytes 9220
  494.8 70.1 %copy-start.36 = (f32[768]{0:T(1024)S(1)}, f32[768]{0:T(1024)}, u32[]{:S(2)}) copy-start(f32[768]{0:T(1024)} %get-tuple-element.636) | copy-start | bytes 9220
  (39 other events, 354.8 us)
Sparse Core Ops, SparseCore 0:
  13.0 39.7 all-gather.5
  118.2 59.3 reduce-scatter.10
  381.1 36.8 all-gather.13
  474.3 89.0 reduce-scatter.16
  567.1 42.3 reduce-scatter.26
  613.3 42.4 reduce-scatter.28
  659.5 34.9 reduce-scatter.24
  698.2 34.9 reduce-scatter.18
  736.9 34.9 reduce-scatter.20
  775.5 34.9 reduce-scatter.22
Sparse Core Ops, SparseCore 1:
  120.4 22.7 all-gather.9
  180.8 36.7 all-gather.7
  219.3 22.7 all-gather.11
  252.5 60.4 reduce-scatter.14
  315.3 60.2 reduce-scatter.12
where the time goes:
time: 820 us; the launch traced here: 818 us
  waiting for transfers between devices  553 us (67%)
  blocking collectives  92.1 us (11%)
  matrix products  79.1 us (10%)
  other arithmetic  40.3 us (5%)
  local copies, waits for them, and re-layouts  27.3 us (3%)
  between operations  16.3 us (2%)
  starting transfers between devices  9.21 us (1%)
    reduce_scatter x1, waiting for transfers between devices, on_device(): lax.psum_scatter(contract_cols(dquery, query_w) + contract_cols(dkey, key...  63.9 us
    reduce_scatter x1, waiting for transfers between devices, on_device(): lax.psum_scatter(jnp.dot(activated, w_down, preferred_element_type=f32),...  59.7 us
    reduce_scatter x1, waiting for transfers between devices, on_device(): lax.psum_scatter(contract_cols(context, out_w), 'tp', scatter_dimension=0...  58.8 us
    reduce_scatter x1, waiting for transfers between devices, on_device(): lax.psum_scatter(jnp.dot(dpreact, w_up, preferred_element_type=f32), 'tp'...  55.6 us
    reduce_scatter x1, waiting for transfers between devices, on_device(): lax.psum_scatter(grad_down_part, 'fsdp', scatter_dimension=0, tiled=True)  46.3 us
    psum x1, blocking collectives, on_device(): lax.psum((grad_gain1, grad_shift1, grad_qbias, grad_vbias, grad_obias, gr...  41.5 us
    reduce_scatter x1, waiting for transfers between devices, on_device(): lax.psum_scatter(grad_key, 'fsdp', scatter_dimension=0, tiled=True)  38.7 us
    reduce_scatter x1, waiting for transfers between devices, on_device(): lax.psum_scatter(grad_query, 'fsdp', scatter_dimension=0, tiled=True)  38.7 us
  transfers between devices with their start and end apart: 19, of which 16 were waited for; matrix products, arithmetic and copies ran while one was open for 6% of the time, Pallas kernels for 0%

commit v1 on v0

--- a/solution.py
+++ b/solution.py
@@ -11,6 +11,28 @@
 root_half = 0.7071067811865476
 inv_root_tau = 0.3989422804014327
 far_negative = -1e30
+
+
+def laid_out(blocks, dim):
+    blocks = jnp.moveaxis(blocks, 0, dim)
+    shape = blocks.shape
+    return blocks.reshape(*shape[:dim], shape[dim] * shape[dim + 1], *shape[dim + 2 :])
+
+
+def collect(x, axis, dim):
+    size = lax.axis_size(axis)
+    pairs = [(i, (i + 1) % size) for i in range(size)]
+    back = [(b, a) for a, b in pairs]
+    lower, upper = ([], [])
+    for turn in range(size - 1):
+        if turn % 2 == 0:
+            lower.append(lax.ppermute(lower[-1] if lower else x, axis, pairs))
+        else:
+            upper.append(lax.ppermute(upper[-1] if upper else x, axis, back))
+    blocks = jnp.stack([*lower[::-1], x, *upper])
+    shift = lax.axis_index(axis) - len(lower)
+    blocks = blocks[(jnp.arange(size) - shift) % size]
+    return laid_out(blocks, dim)
 
 
 def extended(value, sides, width):
@@ -172,7 +194,7 @@
     normed2 = lax.all_gather(normed2_own, "tp", axis=0, tiled=True)
     w_up, w_down = (
         lax.all_gather(fc1_weight, "fsdp", axis=0, tiled=True),
-        lax.all_gather(fc2_weight, "fsdp", axis=0, tiled=True),
+        collect(fc2_weight, "fsdp", 0),
     )
     unit_count = fc1_weight.shape[0]
     bias_up = lax.dynamic_index_in_dim(

time: 820 us -> 794 us (0.968)
  waiting for transfers between devices: 553 us -> 511 us
  local copies, waits for them, and re-layouts: 27.3 us -> 42.9 us
    all_gather x1, waiting for transfers between devices: 33.2 us -> 7 us  [on_device(): normed2 = lax.all_gather(normed2_own, 'tp', axis=0, tiled=True)]
    all_gather x1 -> x0, waiting for transfers between devices: 19.1 us -> none  [on_device(): lax.all_gather(fc2_weight, 'fsdp', axis=0, tiled=True)]
    unnamed x76 -> x85, local copies, waits for them, and re-layouts: 4.8 us -> 17.9 us
    ppermute x0 -> x7, waiting for transfers between devices: none -> 9.52 us  [the longest x4 5.44 us: collect(): lower.append(lax.ppermute(lower[-1] if lower else x, axis, pairs))]
  transfers between devices with their start and end apart: 19 -> 25, of which waited for: 16 -> 17; matrix products, arithmetic and copies ran while one was open for 6% -> 7% of each run, Pallas kernels for 0% -> 0%
where the time goes in v1:
time: 794 us; the launch traced here: 792 us
  waiting for transfers between devices  511 us (64%)
  blocking collectives  92.1 us (12%)
  matrix products  74.1 us (9%)
  local copies, waits for them, and re-layouts  42.9 us (5%)
  other arithmetic  39.6 us (5%)
  between operations  16.3 us (2%)
  starting transfers between devices  16.1 us (2%)
    reduce_scatter x1, waiting for transfers between devices, on_device(): lax.psum_scatter(contract_cols(dquery, query_w) + contract_cols(dkey, key...  64.7 us
    reduce_scatter x1, waiting for transfers between devices, on_device(): lax.psum_scatter(jnp.dot(activated, w_down, preferred_element_type=f32),...  59.7 us
    reduce_scatter x1, waiting for transfers between devices, on_device(): lax.psum_scatter(jnp.dot(dpreact, w_up, preferred_element_type=f32), 'tp'...  54.5 us
    reduce_scatter x1, waiting for transfers between devices, on_device(): lax.psum_scatter(contract_cols(context, out_w), 'tp', scatter_dimension=0...  53 us
    reduce_scatter x1, waiting for transfers between devices, on_device(): lax.psum_scatter(grad_down_part, 'fsdp', scatter_dimension=0, tiled=True)  46.3 us
    psum x1, blocking collectives, on_device(): lax.psum((grad_gain1, grad_shift1, grad_qbias, grad_vbias, grad_obias, gr...  41.5 us
    reduce_scatter x1, waiting for transfers between devices, on_device(): lax.psum_scatter(grad_key, 'fsdp', scatter_dimension=0, tiled=True)  38.7 us
    reduce_scatter x1, waiting for transfers between devices, on_device(): lax.psum_scatter(grad_out, 'fsdp', scatter_dimension=0, tiled=True)  38.7 us
  transfers between devices with their start and end apart: 25, of which 17 were waited for; matrix products, arithmetic and copies ran while one was open for 7% of the time, Pallas kernels for 0%

profile of v1, /device:TPU:0, one launch (start us, length us, event | category | flops | bytes accessed | tf_op | source)
XLA Modules:
  0.0 792.5 jit_solution(7327658905034914366)
XLA Ops:
  13.7 11.0 %all_gather.29 = bf16[768,192]{1,0:T(8,128)(2,1)S(1)} all-gather(bf16[96,192]{1,0:T(8,128)(2,1)S(1)} %copy-done.23), channel_id=1, replica_groups=mesh['fsdp'=8,'tp'=4] {'fsdp'}, dimensions={0}, use_global_device_ids=true | all-gather | bytes 331776 | tf_op jit(solution)/shard_map/all_gather | solution.py:94
  24.7 9.5 %all_gather.30 = bf16[768,192]{1,0:T(8,128)(2,1)S(1)} all-gather(bf16[96,192]{1,0:T(8,128)(2,1)S(1)} %copy-done.24), channel_id=1, replica_groups=mesh['fsdp'=8,'tp'=4] {'fsdp'}, dimensions={0}, use_global_device_ids=true | all-gather | bytes 331776 | tf_op jit(solution)/shard_map/all_gather | solution.py:95
  34.3 18.5 %all-gather.5.cloned.1.call-done = bf16[1024,768]{1,0:T(8,128)(2,1)} async-done(((bf16[256,768]{1,0:T(8,128)(2,1)}), bf16[1024,768]{1,0:T(8,128)(2,1)}) %all-gather.5.cloned.1.call-update) | async-done | bytes 1572880 | tf_op jit(solution)/shard_map/all_gather | solution.py:133
  57.9 4.0 collective-permute-start
  62.7 18.6 %all_gather.31 = bf16[768,192]{1,0:T(8,128)(2,1)S(1)} all-gather(bf16[96,192]{1,0:T(8,128)(2,1)S(1)} %copy-done.25), channel_id=1, replica_groups=mesh['fsdp'=8,'tp'=4] {'fsdp'}, dimensions={0}, use_global_device_ids=true | all-gather | bytes 331776 | tf_op jit(solution)/shard_map/all_gather | solution.py:93
  81.2 11.4 %all_gather.32 = bf16[768,192]{1,0:T(8,128)(2,1)} all-gather(bf16[96,192]{1,0:T(8,128)(2,1)S(1)} %copy-done.26), channel_id=1, replica_groups=mesh['fsdp'=8,'tp'=4] {'fsdp'}, dimensions={0}, use_global_device_ids=true | all-gather | bytes 331776 | tf_op jit(solution)/shard_map/all_gather | solution.py:96
  95.7 17.6 %while.40 = (s32[]{:T(128)}, bf16[1024,192]{0,1:T(8,128)(2,1)}, f32[3,1024]{1,0:T(4,128)S(1)}, s32[]{:T(128)}, bf16[2,3072,192]{1,2,0:T(8,128)(2,1)S(1)}, /*inde...) while((s32[]{:T(128)}, bf16[1024,192]{0,1:T(8,128)(2,1)}, ...), condition=%wide.region_6.7_spmd.clone, body=%wide.region_2.6_spmd.clone.sunk | while | flops 630030336 | bytes 36239832 | solution.py:182
  113.3 3.4 fusion.42
  117.7 5.4 collective-permute-done.2
  123.2 53.0 %reduce-scatter.11.cloned.1.call-done = f32[256,768]{1,0:T(8,128)} async-done(((f32[1024,768]{1,0:T(8,128)}), f32[256,768]{1,0:T(8,128)}) %reduce-scatter.11.cloned.1.call-update) | async-done | bytes 786448 | tf_op jit(solution)/shard_map/reduce_scatter | solution.py:188
  180.9 4.1 collective-permute-done.6
  209.2 7.0 all-gather.7.cloned.1.call-done
  216.2 4.7 multiply_convert_fusion.1
  228.1 4.8 fusion.43
  233.0 54.5 %reduce-scatter.15.cloned.1.call-done = f32[256,768]{1,0:T(8,128)} async-done(((f32[1024,768]{1,0:T(8,128)}), f32[256,768]{1,0:T(8,128)}) %reduce-scatter.15.cloned.1.call-update) | async-done | bytes 786448 | tf_op jit(solution)/shard_map/reduce_scatter | solution.py:219
  290.5 59.7 %reduce-scatter.13.cloned.1.call-done = f32[256,768]{1,0:T(8,128)} async-done(((f32[1024,768]{1,0:T(8,128)}), f32[256,768]{1,0:T(8,128)}) %reduce-scatter.13.cloned.1.call-update) | async-done | bytes 786448 | tf_op jit(solution)/shard_map/reduce_scatter | solution.py:205
  350.1 3.7 fusion.37
  355.6 37.0 %all-gather.11.cloned.1.call-done = bf16[1024,768]{1,0:T(8,128)(2,1)} async-done(((bf16[256,768]{1,0:T(8,128)(2,1)}), bf16[1024,768]{1,0:T(8,128)(2,1)}) %all-gather.11.cloned.1.call-update) | async-done | bytes 1572880 | tf_op jit(solution)/shard_map/all_gather | solution.py:234
  392.5 3.3 convert_multiply_fusion
  400.5 32.3 %while.41 = (s32[]{:T(128)}, bf16[1024,192]{0,1:T(8,128)(2,1)}, f32[2,3072,192]{1,2,0:T(8,128)}, s32[]{:T(128)}, bf16[2,3072,192]{1,2,0:T(8,128)(2,1)S(1)}, /*in...) while((s32[]{:T(128)}, bf16[1024,192]{0,1:T(8,128)(2,1)}, ...), condition=%wide.region_17.18_spmd.clone, body=%wide.region_15.17_spmd.clone.sunk | while | flops 1537181184 | bytes 94420032 | solution.py:268
  407.7 3.4 multiply_convert_fusion.3
  423.9 3.4 multiply_convert_fusion.3
  439.3 4.0 collective-permute-done.10
  450.0 4.3 fusion.48
  455.8 4.7 fusion.29
  473.1 64.7 %reduce-scatter.17.cloned.1.call-done = f32[256,768]{1,0:T(8,128)} async-done(((f32[1024,768]{1,0:T(8,128)}), f32[256,768]{1,0:T(8,128)}) %reduce-scatter.17.cloned.1.call-update) | async-done | bytes 786448 | tf_op jit(solution)/shard_map/reduce_scatter | solution.py:286
  539.4 41.5 %all-reduce = (f32[768]{0:T(1024)}, f32[768]{0:T(1024)}, f32[768]{0:T(1024)}, f32[768]{0:T(1024)}, f32[768]{0:T(1024)}, /*index=5*/f32[768]{0:T(1024)}, f32[768]{0:T(1024)}, f32[3072]{0:T(1024)}, f32[768]{0:T(1024)}) all-reduce(f32[768]{0:T(1024)S(1)} %get-tuple-element.569, ...), channel_id=1, replica_groups=mesh['fsdp'=8,'tp'=4] {'fsdp','tp'}, use_global_device_ids=true, to_apply=%region_22.23 | all-reduce | flops 9216 | bytes 73728 | tf_op jit(solution)/shard_map/psum | solution.py:313
  584.0 46.3 %reduce-scatter.29.cloned.1.call-done = f32[96,768]{1,0:T(8,128)} async-done(((f32[768,768]{1,0:T(8,128)}), f32[96,768]{1,0:T(8,128)}) %reduce-scatter.29.cloned.1.call-update) | async-done | bytes 294928 | tf_op jit(solution)/shard_map/reduce_scatter | solution.py:224
  630.3 38.7 %reduce-scatter.25.cloned.1.call-done = f32[96,192]{1,0:T(8,128)} async-done(((f32[768,192]{1,0:T(8,128)}), f32[96,192]{1,0:T(8,128)}) %reduce-scatter.25.cloned.1.call-update) | async-done | bytes 73744 | tf_op jit(solution)/shard_map/reduce_scatter | solution.py:301
  669.0 38.7 %reduce-scatter.19.cloned.1.call-done = f32[96,192]{1,0:T(8,128)} async-done(((f32[768,192]{1,0:T(8,128)}), f32[96,192]{1,0:T(8,128)}) %reduce-scatter.19.cloned.1.call-update) | async-done | bytes 73744 | tf_op jit(solution)/shard_map/reduce_scatter | solution.py:298
  707.7 38.7 %reduce-scatter.21.cloned.1.call-done = f32[96,192]{1,0:T(8,128)} async-done(((f32[768,192]{1,0:T(8,128)}), f32[96,192]{1,0:T(8,128)}) %reduce-scatter.21.cloned.1.call-update) | async-done | bytes 73744 | tf_op jit(solution)/shard_map/reduce_scatter | solution.py:299
  746.4 38.5 %reduce-scatter.23.cloned.1.call-done = f32[96,192]{1,0:T(8,128)} async-done(((f32[768,192]{1,0:T(8,128)}), f32[96,192]{1,0:T(8,128)}) %reduce-scatter.23.cloned.1.call-update) | async-done | bytes 73744 | tf_op jit(solution)/shard_map/reduce_scatter | solution.py:300
  (259 shorter events, 135.3 us)
Async XLA Ops:
  8.0 44.7 %all-gather.5.cloned.1.call-start = ((), (), s32[]{:S(2)}) async-start(), calls=%async_computation.10 | async-start | bytes 1966080 | tf_op jit(solution)/shard_map/all_gather | solution.py:133
  12.9 163.3 %reduce-scatter.11.cloned.1.call-start = ((), (), s32[]{:S(2)}) async-start(), calls=%async_computation.11 | async-start | bytes 3932160 | tf_op jit(solution)/shard_map/reduce_scatter | solution.py:188
  56.6 36.7 %collective-permute-start.1 = (bf16[2,1024,192]{1,2,0:T(8,128)(2,1)}, bf16[2,1024,192]{1,2,0:T(8,128)(2,1)}, u32[]{:S(2)}, u32[]{:S(2)}) collective-permute-start(bf16[2,1024,192]{1,2,0:T(8,128)(2,1)} %pad_maximum_fusion.1), channel_id=1, source_target_pairs={{4,0},{8,4},{12,8},{16,12},{20,16},{24,20},{28,24},{5,1},{9,5},{13... | collective-permute-start | bytes 2359304 | tf_op jit(solution)/shard_map/ppermute | solution.py:46
  57.9 35.4 %collective-permute-start = (bf16[2,1024,192]{1,2,0:T(8,128)(2,1)}, bf16[2,1024,192]{1,2,0:T(8,128)(2,1)}, u32[]{:S(2)}, u32[]{:S(2)}) collective-permute-start(bf16[2,1024,192]{1,2,0:T(8,128)(2,1)} %pad_maximum_fusion.1), channel_id=1, source_target_pairs={{0,4},{4,8},{8,12},{12,16},{16,20},{20,24},{24,28},{1,5},{5,9},{9,... | collective-permute-start | bytes 2359304 | tf_op jit(solution)/shard_map/ppermute | solution.py:45
  116.7 92.5 %all-gather.9.cloned.1.call-start = ((), (), s32[]{:S(2)}) async-start(), calls=%async_computation.13 | async-start | bytes 1327104 | tf_op jit(solution)/shard_map/all_gather | solution.py:196
  117.3 98.9 %all-gather.7.cloned.1.call-start = ((), (), s32[]{:S(2)}) async-start(), calls=%async_computation.12 | async-start | bytes 1966080 | tf_op jit(solution)/shard_map/all_gather | solution.py:194
  117.3 5.8 collective-permute-start.2
  123.2 57.7 %collective-permute-start.3 = (bf16[96,768]{1,0:T(8,128)(2,1)}, bf16[96,768]{1,0:T(8,128)(2,1)}, u32[]{:S(2)}, u32[]{:S(2)}) collective-permute-start(bf16[96,768]{1,0:T(8,128)(2,1)} %collective-permute-done.2), channel_id=1, source_target_pairs={{0,4},{4,8},{8,12},{12,16},{16,20},{20,24},{24,28},{28,0},{1,5},{5... | collective-permute-start | bytes 442376 | tf_op jit(solution)/shard_map/ppermute | solution.py:29
  179.4 108.2 %reduce-scatter.15.cloned.1.call-start = ((), (), s32[]{:S(2)}) async-start(), calls=%async_computation.15 | async-start | bytes 3932160 | tf_op jit(solution)/shard_map/reduce_scatter | solution.py:219
  179.4 5.6 collective-permute-start.6
  180.9 6.9 collective-permute-start.4
  185.0 6.8 collective-permute-start.7
  187.8 6.6 collective-permute-start.5
  191.8 13.8 %collective-permute-start.8 = (bf16[96,768]{1,0:T(8,128)(2,1)}, bf16[96,768]{1,0:T(8,128)(2,1)S(1)}, u32[]{:S(2)}, u32[]{:S(2)}) collective-permute-start(bf16[96,768]{1,0:T(8,128)(2,1)} %collective-permute-done.7), channel_id=1, source_target_pairs={{4,0},{8,4},{12,8},{16,12},{20,16},{24,20},{28,24},{0,28},{5,1},{9... | collective-permute-start | bytes 442376 | tf_op jit(solution)/shard_map/ppermute | solution.py:31
  228.1 122.0 %reduce-scatter.13.cloned.1.call-start = ((), (), s32[]{:S(2)}) async-start(), calls=%async_computation.14 | async-start | bytes 3932160 | tf_op jit(solution)/shard_map/reduce_scatter | solution.py:205
  233.0 159.5 %all-gather.11.cloned.1.call-start = ((), (), s32[]{:S(2)}) async-start(), calls=%async_computation.16 | async-start | bytes 1966080 | tf_op jit(solution)/shard_map/all_gather | solution.py:234
  355.5 182.3 %reduce-scatter.17.cloned.1.call-start = ((), (), s32[]{:S(2)}) async-start(), calls=%async_computation.17 | async-start | bytes 3932160 | tf_op jit(solution)/shard_map/reduce_scatter | solution.py:286
  435.0 4.3 collective-permute-start.9
  436.4 6.9 collective-permute-start.10
  448.7 135.3 %reduce-scatter.27.cloned.1.call-start = ((), (), s32[]{:S(2)}) async-start(), calls=%async_computation.22 | async-start | bytes 2654208 | tf_op jit(solution)/shard_map/reduce_scatter | solution.py:223
  454.4 175.9 %reduce-scatter.29.cloned.1.call-start = ((), (), s32[]{:S(2)}) async-start(), calls=%async_computation.23 | async-start | bytes 2654208 | tf_op jit(solution)/shard_map/reduce_scatter | solution.py:224
  460.5 208.5 %reduce-scatter.25.cloned.1.call-start = ((), (), s32[]{:S(2)}) async-start(), calls=%async_computation.21 | async-start | bytes 884736 | tf_op jit(solution)/shard_map/reduce_scatter | solution.py:301
  464.4 243.3 %reduce-scatter.19.cloned.1.call-start = ((), (), s32[]{:S(2)}) async-start(), calls=%async_computation.18 | async-start | bytes 884736 | tf_op jit(solution)/shard_map/reduce_scatter | solution.py:298
  466.1 280.3 %reduce-scatter.21.cloned.1.call-start = ((), (), s32[]{:S(2)}) async-start(), calls=%async_computation.19 | async-start | bytes 884736 | tf_op jit(solution)/shard_map/reduce_scatter | solution.py:299
  468.8 69.1 %copy-start.27 = (f32[768]{0:T(1024)S(1)}, f32[768]{0:T(1024)}, u32[]{:S(2)}) copy-start(f32[768]{0:T(1024)} %param.33) | copy-start | bytes 9220
  468.8 69.1 %copy-start.30 = (f32[256]{0:T(256)S(1)}, f32[256]{0:T(256)}, u32[]{:S(2)}) copy-start(f32[256]{0:T(256)} %copy-done.29) | copy-start | bytes 3076
  468.8 69.1 %copy-start.32 = (f32[256]{0:T(256)S(1)}, f32[256]{0:T(256)}, u32[]{:S(2)}) copy-start(f32[256]{0:T(256)} %copy-done.31) | copy-start | bytes 3076
  468.8 316.1 %reduce-scatter.23.cloned.1.call-start = ((), (), s32[]{:S(2)}) async-start(), calls=%async_computation.20 | async-start | bytes 884736 | tf_op jit(solution)/shard_map/reduce_scatter | solution.py:300
  470.5 68.9 %copy-start.34 = (f32[768]{0:T(1024)S(1)}, f32[768]{0:T(1024)}, u32[]{:S(2)}) copy-start(f32[768]{0:T(1024)} %get-tuple-element.573) | copy-start | bytes 9220
  470.5 68.9 %copy-start.35 = (f32[768]{0:T(1024)S(1)}, f32[768]{0:T(1024)}, u32[]{:S(2)}) copy-start(f32[768]{0:T(1024)} %get-tuple-element.620) | copy-start | bytes 9220
  470.5 68.9 %copy-start.36 = (f32[768]{0:T(1024)S(1)}, f32[768]{0:T(1024)}, u32[]{:S(2)}) copy-start(f32[768]{0:T(1024)} %get-tuple-element.636) | copy-start | bytes 9220
  470.5 110.5 %copy-start.6 = (f32[256,768]{1,0:T(8,128)S(1)}, f32[256,768]{1,0:T(8,128)}, u32[]{:S(2)}) copy-start(f32[256,768]{1,0:T(8,128)} %copy-done.5) | copy-start | bytes 2359300
  (46 other events, 527.4 us)
Sparse Core Ops, SparseCore 0:
  13.0 39.7 all-gather.4
  116.8 59.3 reduce-scatter.10
  355.6 36.8 all-gather.10
  448.8 89.0 reduce-scatter.16
  541.6 42.3 reduce-scatter.26
  587.8 42.4 reduce-scatter.28
  634.0 34.9 reduce-scatter.24
  672.7 34.9 reduce-scatter.18
  711.4 34.9 reduce-scatter.20
  749.9 34.9 reduce-scatter.22
Sparse Core Ops, SparseCore 1:
  119.1 22.7 all-gather.8
  179.4 36.7 all-gather.6
  228.2 59.3 reduce-scatter.14
  289.8 60.2 reduce-scatter.12
